TPU v7x, 32 devices: a whole 2x2x4 slice. The times are simulated.
32 devices in a mesh: blk: 8 (over y, x, core), chan: 4 (over z).
Axes of the slice: x: 2, y: 2, z: 4, core: 2. Of those that a mesh axis runs over, the one named last changes fastest.
Arguments:
- pair_repr: bfloat16 [512, 512, 128], P('blk', 'chan'), may hold values from -6 to 6
- chain_lengths: int32 [8], replicated, may hold values from 48 to 64
- norm_gain: float32 [128], replicated, may hold values from 0.1 to 1.9
- norm_bias: float32 [128], replicated, may hold values from -3 to 3
- left_gate: bfloat16 [128, 128], replicated, may hold values from -0.5 to 0.5
- left_value: bfloat16 [128, 128], replicated, may hold values from -0.5 to 0.5
- right_gate: bfloat16 [128, 128], replicated, may hold values from -0.5 to 0.5
- right_value: bfloat16 [128, 128], replicated, may hold values from -0.5 to 0.5
- out_gain: float32 [128], replicated, may hold values from 0.1 to 1.9
- out_bias: float32 [128], replicated, may hold values from -3 to 3
- out_weight: bfloat16 [128, 128], replicated, may hold values from -0.5 to 0.5
- gate_weight: bfloat16 [128, 128], replicated, may hold values from -0.5 to 0.5
Outputs:
- pair_update: bfloat16 [512, 104, 128], P('blk', 'chan')
Inputs may be any that keep to these rules, and one draw needn't show every extreme that they name: Chain slot s covers residues s * 64 to (s + 1) * 64 - 1, of which the first chain_lengths[s] are real and the rest padding.
All inputs are finite; a program needn't handle non-finite values.
Results may differ from a plain program's by a relative error of at most 0.0058.
Values may be sent and summed in bfloat16 or wider, within the bound.
A program may use at most 64 MiB of HBM per device.

v0:
```python
import jax
import jax.numpy as jnp
from jax import lax
from jax.sharding import PartitionSpec as P

JD = 13


epsilon = 1e-05


def normalize(values, gain_vec, bias_vec):
    centre = jnp.mean(values, axis=-1, keepdims=True)
    centred = values - centre
    spread_sq = jnp.mean(centred * centred, axis=-1, keepdims=True)
    return centred * lax.rsqrt(spread_sq + epsilon) * gain_vec + bias_vec


def residue_mask(position, lengths, slot_size):
    chain_id = position // slot_size
    chain_table = jnp.arange(lengths.shape[0], dtype=jnp.int32)
    chain_len = jnp.sum(
        jnp.where(chain_id[:, None] == chain_table[None, :], lengths[None, :], 0), axis=1
    )
    return (position % slot_size < chain_len).astype(jnp.float32)


def on_device(
    pair_repr,
    chain_lengths,
    norm_gain,
    norm_bias,
    left_gate,
    left_value,
    right_gate,
    right_value,
    out_gain,
    out_bias,
    out_weight,
    gate_weight,
):
    row_count = pair_repr.shape[0]
    col_count = pair_repr.shape[1]
    hidden = left_gate.shape[1]
    cycle_size = lax.axis_size("blk")
    cycle_index = lax.axis_index("blk")
    residues = row_count * cycle_size
    slot_size = residues // chain_lengths.shape[0]
    row_start = cycle_index * row_count
    col_start = lax.axis_index("chan") * col_count
    row_real = residue_mask(
        row_start + jnp.arange(row_count, dtype=jnp.int32), chain_lengths, slot_size
    )
    col_real = residue_mask(
        col_start + jnp.arange(col_count, dtype=jnp.int32), chain_lengths, slot_size
    )
    normed = normalize(pair_repr.astype(jnp.float32), norm_gain, norm_bias).astype(jnp.bfloat16)
    left_stack = jnp.concatenate([left_gate, left_value], axis=1)
    left_mix = jnp.einsum("ikd,de->eik", normed, left_stack, preferred_element_type=jnp.float32)
    left_proj = (
        jax.nn.sigmoid(left_mix[:hidden])
        * left_mix[hidden:]
        * (row_real[:, None] * col_real[None, :])
    ).astype(jnp.bfloat16)
    right_stack = jnp.concatenate([right_gate, right_value], axis=1)
    right_mix = jnp.einsum(
        "jkd,de->ejk", normed[:JD], right_stack, preferred_element_type=jnp.float32
    )
    right_proj = (
        jax.nn.sigmoid(right_mix[:hidden])
        * right_mix[hidden:]
        * (row_real[:JD, None] * col_real[None, :])
    ).astype(jnp.bfloat16)
    left_all, right_all = (
        lax.all_to_all(left_proj, "chan", split_axis=0, concat_axis=2, tiled=True),
        lax.all_to_all(right_proj, "chan", split_axis=0, concat_axis=2, tiled=True),
    )
    window = right_all.shape[1]
    product = jnp.einsum(
        "cik,cjk->cij",
        left_all,
        lax.all_gather(right_all, "blk", axis=1, tiled=True),
        preferred_element_type=jnp.float32,
    )
    column_slab = lax.all_to_all(
        product.astype(jnp.bfloat16), "chan", split_axis=2, concat_axis=0, tiled=True
    )
    values = column_slab.astype(jnp.float32)
    centre = jnp.mean(values, axis=0, keepdims=True)
    centred = values - centre
    spread_sq = jnp.mean(centred * centred, axis=0, keepdims=True)
    normed_product = (
        centred * lax.rsqrt(spread_sq + epsilon) * out_gain[:, None, None] + out_bias[:, None, None]
    ).astype(jnp.bfloat16)
    update = jnp.einsum(
        "cij,cd->ijd", normed_product, out_weight, preferred_element_type=jnp.float32
    )
    gate_rows = jnp.concatenate(
        [normed[:, :window], normed[:, row_count : row_count + window]], axis=1
    )
    gate_value = jax.nn.sigmoid(
        jnp.einsum("ijd,de->ije", gate_rows, gate_weight, preferred_element_type=jnp.float32)
    )
    return (gate_value * update).astype(jnp.bfloat16)


def solution(mesh):
    in_specs = (P("blk", "chan", None), P(), P(), P(), P(), P(), P(), P(), P(), P(), P(), P())
    out_specs = P("blk", "chan", None)
    return jax.shard_map(
        on_device, mesh=mesh, in_specs=in_specs, out_specs=out_specs, check_vma=False
    )
```

profile of v0, /device:TPU:0, one launch (start us, length us, event | category | flops | bytes accessed | tf_op | source)
XLA Modules:
  0.0 144.4 jit_solution(7111051878414776538)
XLA Ops:
  6.6 0.9 select_reduce_fusion.1
  7.5 0.7 select_reduce_fusion
  8.2 0.0 copy-start.10
  8.2 3.5 %convert_reduce_fusion = f32[64,128]{0,1:T(8,128)S(1)} fusion(bf16[64,128,128]{2,1,0:T(8,128)(2,1)} %param.12), kind=kLoop, calls=%fused_computation.1 | loop fusion | flops 2088960 | bytes 2129920 | tf_op jit(solution)/shard_map/reduce_sum | solution.py:13
  11.8 7.1 %fusion.2 = f32[64,128]{0,1:T(8,128)S(1)} fusion(f32[64,128]{0,1:T(8,128)S(1)} %broadcast_multiply_fusion, bf16[64,128,128]{2,1,0:T(8,128)(2,1)S(1)} %copy-done.1), kind=kLoop, calls=%fused_computation.4 | loop fusion | flops 4186112 | bytes 2162688 | tf_op jit(solution)/shard_map/reduce_sum | solution.py:15
  18.9 0.0 copy-start.5
  18.9 0.0 copy-start.6
  18.9 5.4 %fusion.5 = bf16[64,128,128]{2,0,1:T(8,128)(2,1)S(1)} fusion(f32[128]{0:T(128)S(1)} %copy-done.9, f32[128]{0:T(128)S(1)} %copy-done.10, f32[64,128]{0,1:T(8,128)S(1)} %add_rsqrt_fusion, f32[64,128]{0,1:T(8,128)S(1)} %broadcast_multiply_fusion, bf16[64,128,128]{2,1,0:T(8,128)(2,1)S(1)} %copy-done.1), kind=kLoop, calls=%fused_computation.7 | loop fusion | flops 6291456 | bytes 4260864 | tf_op jit(solution)/shard_map/convert_element_type | solution.py:57
  24.3 1.3 copy-done.2
  25.7 0.1 slice.36
  25.7 0.1 copy.58
  25.9 0.1 copy.59
  26.0 0.1 broadcast_multiply_fusion.3
  26.1 0.4 fusion.35
  26.5 0.2 fusion.28
  26.7 0.0 copy-start.7
  26.7 0.0 copy-start.8
  26.7 0.3 copy.61
  27.0 20.8 %all_to_all.45 = bf16[128,13,128]{2,1,0:T(8,128)(2,1)S(1)} all-to-all(bf16[128,13,128]{2,1,0:T(8,128)(2,1)S(1)} %copy.61), channel_id=1, replica_groups=mesh['blk'=8,'chan'=4] {'chan'}, dimensions={0} | all-to-all | bytes 851968 | tf_op jit(solution)/shard_map/all_to_all | solution.py:76
  47.8 0.3 copy.82
  48.2 0.9 all_to_all.40
  49.1 0.0 all-gather.2.cloned.1.call-update
  49.1 0.1 copy.53
  49.2 0.1 copy.54
  49.4 0.1 broadcast_multiply_fusion.1
  49.4 1.9 %fusion.13 = f32[256,64,128]{2,0,1:T(8,128)S(1)} fusion(bf16[64,128,128]{2,0,1:T(8,128)(2,1)S(1)} %copy-done.3, bf16[128,128]{0,1:T(8,128)(2,1)S(1)} %copy.54, bf16[128,128]{0,1:T(8,128)(2,1)S(1)} %copy.53), kind=kOutput, calls=%fused_computation.18 | convolution fusion | flops 537001984 | bytes 10551296 | tf_op jit(solution)/shard_map/ikd,de->eik/dot_general | solution.py:59
  51.3 1.2 fusion.7
  52.6 1.4 copy.56
  53.9 50.3 %all_to_all.46 = bf16[128,64,128]{2,1,0:T(8,128)(2,1)S(1)} all-to-all(bf16[128,64,128]{2,1,0:T(8,128)(2,1)S(1)} %copy.56), channel_id=1, replica_groups=mesh['blk'=8,'chan'=4] {'chan'}, dimensions={0} | all-to-all | bytes 4194304 | tf_op jit(solution)/shard_map/all_to_all | solution.py:75
  104.2 3.3 %copy.81 = bf16[4,32,64,128]{3,0,2,1:T(4,128)(2,1)} copy(bf16[4,32,64,128]{3,2,1,0:T(8,128)(2,1)S(1)} %bitcast.48) | data formatting | bytes 4194304 | tf_op jit(solution)/shard_map/all_to_all | solution.py:75
  107.5 4.1 %all_to_all.36 = bf16[32,64,512]{2,1,0:T(8,128)(2,1)} reshape(bf16[32,64,4,128]{3,2,1,0:T(4,128)(2,1)} %bitcast.49) | data formatting | bytes 4194304 | tf_op jit(solution)/shard_map/all_to_all | solution.py:75
  111.7 4.8 %fusion.22 = bf16[32,64,104]{2,1,0:T(8,128)(2,1)S(1)} fusion(bf16[32,64,512]{2,1,0:T(8,128)(2,1)} %all_to_all.36, bf16[32,104,512]{2,0,1:T(8,128)(2,1)} %all-gather.2.cloned.1.call-done), kind=kOutput, calls=%fused_computation.32 | convolution fusion | flops 218316800 | bytes 5931008 | tf_op jit(solution)/shard_map/cik,cjk->cij/dot_general | solution.py:79
  116.4 1.3 copy.64
  117.8 1.4 reshape.169
  119.1 3.5 %all-to-all-start.2 = ((bf16[4,2,26624]{2,1,0:T(2,128)(2,1)}), bf16[4,2,26624]{2,1,0:T(2,128)(2,1)S(1)}, u32[]{:S(2)}, u32[]{:S(2)}) async-start(bf16[4,2,26624]{2,1,0:T(2,128)(2,1)} %reshape.169), calls=%async_computation.2 | async-start | bytes 851968 | tf_op jit(solution)/shard_map/all_to_all | solution.py:85
  122.7 0.4 fusion.21
  123.0 10.9 %all-to-all-done.2 = bf16[4,2,26624]{2,1,0:T(2,128)(2,1)S(1)} async-done(((bf16[4,2,26624]{2,1,0:T(2,128)(2,1)}), bf16[4,2,26624]{2,1,0:T(2,128)(2,1)S(1)}, u32[]{:S(2)}, u32[]{:S(2)}) %all-to-all-start.2) | async-done | bytes 426016 | tf_op jit(solution)/shard_map/all_to_all | solution.py:85
  134.0 0.5 reshape.170
  134.5 0.2 fusion.26
  134.7 0.2 convert_bitcast_fusion
  134.9 0.0 copy-start.11
  135.0 0.3 multiply_reduce_fusion
  135.3 0.1 copy.65
  135.4 0.2 copy-done.11
  135.6 0.0 copy-done.12
  135.6 0.4 fusion.18
  136.0 0.4 copy-done.4
  136.4 1.2 fusion.25
  (27 shorter events, 0.2 us)
Async XLA Ops:
  6.5 116.1 %copy-start = (bf16[128,128]{1,0:T(8,128)(2,1)S(1)}, bf16[128,128]{1,0:T(8,128)(2,1)}, u32[]{:S(2)}) copy-start(bf16[128,128]{1,0:T(8,128)(2,1)} %param.23) | copy-start | bytes 98308
  6.5 5.2 %copy-start.1 = (bf16[64,128,128]{2,1,0:T(8,128)(2,1)S(1)}, bf16[64,128,128]{2,1,0:T(8,128)(2,1)}, u32[]{:S(2)}) copy-start(bf16[64,128,128]{2,1,0:T(8,128)(2,1)} %param.12) | copy-start | bytes 6291460
  6.5 105.1 %all-gather.2.cloned.1.call-start = ((), (), s32[]{:S(2)}) async-start(), calls=%async_computation.3 | async-start | bytes 3833856 | tf_op jit(solution)/shard_map/all_gather | solution.py:82
  8.2 10.6 %copy-start.9 = (f32[128]{0:T(128)S(1)}, f32[128]{0:T(128)}, u32[]{:S(2)}) copy-start(f32[128]{0:T(128)} %param.15) | copy-start | bytes 1540
  8.2 10.6 %copy-start.10 = (f32[128]{0:T(128)S(1)}, f32[128]{0:T(128)}, u32[]{:S(2)}) copy-start(f32[128]{0:T(128)} %param.14) | copy-start | bytes 1540
  18.9 6.8 %copy-start.5 = (bf16[128,128]{1,0:T(8,128)(2,1)S(1)}, bf16[128,128]{1,0:T(8,128)(2,1)}, u32[]{:S(2)}) copy-start(bf16[128,128]{1,0:T(8,128)(2,1)} %param.18) | copy-start | bytes 98308
  18.9 7.0 %copy-start.6 = (bf16[128,128]{1,0:T(8,128)(2,1)S(1)}, bf16[128,128]{1,0:T(8,128)(2,1)}, u32[]{:S(2)}) copy-start(bf16[128,128]{1,0:T(8,128)(2,1)} %param.19) | copy-start | bytes 98308
  24.3 1.4 copy-start.2
  26.7 22.4 %copy-start.7 = (bf16[128,128]{1,0:T(8,128)(2,1)S(1)}, bf16[128,128]{1,0:T(8,128)(2,1)}, u32[]{:S(2)}) copy-start(bf16[128,128]{1,0:T(8,128)(2,1)} %param.16) | copy-start | bytes 98308
  26.7 22.5 %copy-start.8 = (bf16[128,128]{1,0:T(8,128)(2,1)S(1)}, bf16[128,128]{1,0:T(8,128)(2,1)}, u32[]{:S(2)}) copy-start(bf16[128,128]{1,0:T(8,128)(2,1)} %param.17) | copy-start | bytes 98308
  26.7 22.7 %copy-start.3 = (bf16[64,128,128]{2,0,1:T(8,128)(2,1)S(1)}, bf16[64,128,128]{2,0,1:T(8,128)(2,1)}, u32[]{:S(2)}) copy-start(bf16[64,128,128]{2,0,1:T(8,128)(2,1)} %copy-done.2) | copy-start | bytes 6291460
  119.1 14.8 %all-to-all-start.2 = ((bf16[4,2,26624]{2,1,0:T(2,128)(2,1)}), bf16[4,2,26624]{2,1,0:T(2,128)(2,1)S(1)}, u32[]{:S(2)}, u32[]{:S(2)}) async-start(bf16[4,2,26624]{2,1,0:T(2,128)(2,1)} %reshape.169), calls=%async_computation.2 | async-start | bytes 851968 | tf_op jit(solution)/shard_map/all_to_all | solution.py:85
  134.9 0.7 copy-start.11
  135.0 0.7 copy-start.12
  135.6 0.8 copy-start.4
Sparse Core Ops, SparseCore 0:
  49.2 32.3 all-gather.1
where the time goes:
time: 145 us; the launch traced here: 144 us
  blocking collectives  71.1 us (49%)
  other arithmetic  20.4 us (14%)
  local copies, waits for them, and re-layouts  16.2 us (11%)
  between operations  13.7 us (9%)
  waiting for transfers between devices  11 us (8%)
  matrix products  8.59 us (6%)
  starting transfers between devices  3.47 us (2%)
    all_to_all x1, blocking collectives, on_device(): lax.all_to_all(left_proj, 'chan', split_axis=0, concat_axis=2, tiled=True)  50.3 us
    all_to_all x1, blocking collectives, on_device(): lax.all_to_all(right_proj, 'chan', split_axis=0, concat_axis=2, tiled=True)  20.8 us
    all_to_all x1, waiting for transfers between devices, on_device(): lax.all_to_all(product.astype(jnp.bfloat16), 'chan', split_axis=2, concat...  10.9 us
    all_to_all x2, local copies, waits for them, and re-layouts, on_device(): lax.all_to_all(left_proj, 'chan', split_axis=0, concat_axis=2, tiled=True)  7.43 us
    reduce_sum x1, other arithmetic, normalize(): spread_sq = jnp.mean(centred * centred, axis=-1, keepdims=True)  7.08 us
    convert_element_type x1, other arithmetic, on_device(): normalize(pair_repr.astype(jnp.float32), norm_gain, norm_bias)  5.38 us
    dot_general x1, matrix products, on_device(): jnp.einsum('cik,cjk->cij', left_all, lax.all_gather(right_all, 'blk', axi...  4.78 us
    unnamed x32, local copies, waits for them, and re-layouts  4.29 us
  transfers between devices with their start and end apart: 2, of which 1 were waited for; matrix products, arithmetic and copies ran while one was open for 6% of the time, Pallas kernels for 0%

commit v1 on v0

v1 whole, which is shorter than its diff:
```python
import functools

import jax
import jax.numpy as jnp
from jax import lax
from jax.experimental import pallas as pl
from jax.experimental.pallas import tpu as pltpu
from jax.sharding import PartitionSpec as P

JD = 13
PAD = 16
EPS = 1e-05
F32 = jnp.float32
BF16 = jnp.bfloat16
NT = (((1,), (1,)), ((), ()))
TN = (((0,), (0,)), ((), ()))
NN = (((1,), (0,)), ((), ()))


def xor(a, b, n):
    total, bit = 0, 1
    while bit < n:
        total = total + bit * ((a // bit + b // bit) % 2)
        bit *= 2
    return total


def sigmoid(x):
    return 0.5 * jnp.tanh(0.5 * x) + 0.5


def layer_norm(x, gain, bias):
    centre = jnp.mean(x, axis=-1, keepdims=True)
    centred = x - centre
    spread = jnp.mean(centred * centred, axis=-1, keepdims=True)
    return centred * lax.rsqrt(spread + EPS) * gain + bias


def kernel(
    n_pos,
    slot_size,
    lens,
    pair_hbm,
    gain,
    bias,
    lgate,
    lvalue,
    rgate,
    rvalue,
    ogain,
    obias,
    oweight,
    gweight,
    out,
    pair,
    weights,
    right_all,
    left,
    r0,
    r1,
    work,
    send,
    recv,
    gate_in,
    gate_val,
    update,
    load_sem,
    rs_send,
    rs_recv,
    fw_send,
    fw_recv,
    ps_send,
    ps_recv,
):
    rows, cols, ch = pair.shape
    hid = lgate.shape[1]
    blk = lax.axis_index("blk")
    z = lax.axis_index("chan")
    q = blk // 2
    h = blk % 2
    partner = 2 * q + 1 - h

    load_a = pltpu.make_async_copy(
        pair_hbm.at[pl.ds(0, JD)], pair.at[pl.ds(0, JD)], load_sem.at[0]
    )
    load_b = pltpu.make_async_copy(
        pair_hbm.at[pl.ds(JD, rows - JD)], pair.at[pl.ds(JD, rows - JD)], load_sem.at[1]
    )
    load_a.start()
    load_b.start()

    barrier = pltpu.get_barrier_semaphore()
    for d in range(1, n_pos):
        pl.semaphore_signal(barrier, inc=1, device_id={"blk": 2 * xor(q, d, n_pos) + h})
        pl.semaphore_signal(barrier, inc=1, device_id={"chan": xor(z, d, n_pos)})
    pl.semaphore_signal(barrier, inc=1, device_id={"blk": partner})

    for n, w in enumerate((rgate, rvalue, lgate, lvalue)):
        weights[n * hid : (n + 1) * hid, :] = w[...].astype(F32).T.astype(BF16)

    col = z * cols + lax.broadcasted_iota(jnp.int32, (1, cols), 1)
    chain = col // slot_size
    chain_len = jnp.zeros_like(col)
    for s in range(lens.shape[0]):
        chain_len = jnp.where(chain == s, lens[s], chain_len)
    col_real = (col % slot_size < chain_len).astype(F32)

    def row_real(i):
        pos = blk * rows + i
        return jnp.where(pos % slot_size < lens[pos // slot_size], 1.0, 0.0).astype(F32)

    gain_v, bias_v = gain[...], bias[...]

    def norm_rows(i, count):
        x = pair[pl.ds(i, count)].astype(F32).reshape(count * cols, ch)
        return layer_norm(x, gain_v, bias_v).astype(BF16)

    load_a.wait()

    def right_row(m, carry):
        normed = norm_rows(m, 1)
        mix = lax.dot_general(weights[: 2 * hid, :], normed, NT, preferred_element_type=F32)
        val = sigmoid(mix[:hid]) * mix[hid:] * (col_real * row_real(m))
        right_all[blk, pl.ds(pl.multiple_of(m * hid, hid), hid), :] = val.astype(BF16)
        return carry

    lax.fori_loop(0, JD, right_row, 0)

    pl.semaphore_wait(barrier, 2 * (n_pos - 1) + 1)

    def right_copy(d):
        return pltpu.make_async_remote_copy(
            src_ref=right_all.at[blk],
            dst_ref=right_all.at[blk],
            send_sem=rs_send.at[d],
            recv_sem=rs_recv.at[d],
            device_id={"blk": 2 * xor(q, d, n_pos) + h},
        )

    def forward_copy(d):
        mine = 2 * xor(q, d, n_pos) + h
        return pltpu.make_async_remote_copy(
            src_ref=right_all.at[mine],
            dst_ref=right_all.at[mine],
            send_sem=fw_send.at[d],
            recv_sem=fw_recv.at[d],
            device_id={"blk": partner},
        )

    forward_copy(0).start()
    for d in range(1, n_pos):
        right_copy(d).start()

    load_b.wait()

    def left_rows(t, carry):
        i = 2 * t
        normed = norm_rows(i, 2)
        for u in range(2):
            for g in range(2):
                gate_in[g, i + u] = normed[u * cols + g * rows : u * cols + g * rows + PAD]
        mix = lax.dot_general(weights[2 * hid :, :], normed, NT, preferred_element_type=F32)
        val = sigmoid(mix[:hid]) * mix[hid:]
        for u in range(2):
            left[pl.ds(i + u, hid, stride=rows), :] = val[:, u * cols : (u + 1) * cols] * (
                col_real * row_real(i + u)
            )
        return carry

    lax.fori_loop(0, rows // 2, left_rows, 0)

    zero_rows = jnp.zeros((hid, cols), F32)
    for m in range(JD, PAD):
        r0[pl.ds(m, hid, stride=PAD), :] = zero_rows
        r1[pl.ds(m, hid, stride=PAD), :] = zero_rows

    def partial_copy(p):
        e = xor(z, p, n_pos)
        return pltpu.make_async_remote_copy(
            src_ref=send.at[p],
            dst_ref=recv.at[e],
            send_sem=ps_send.at[e],
            recv_sem=ps_recv.at[e],
            device_id={"chan": p},
        )

    def stage(d, carry):
        p = xor(q, d, n_pos)

        @pl.when(d > 0)
        def _():
            right_copy(d).wait_recv()
            forward_copy(d).start()

        forward_copy(d).wait_recv()
        for g, dst in enumerate((r0, r1)):
            for m in range(JD):
                dst[pl.ds(m, hid, stride=PAD), :] = right_all[
                    2 * p + g, m * hid : (m + 1) * hid, :
                ].astype(F32)

        def channels(t, inner):
            for u in range(8):
                c = 8 * t + u
                rr = pl.ds(pl.multiple_of(c * PAD, PAD), PAD)
                lhs = jnp.concatenate([r0[rr, :], r1[rr, :]], axis=1).astype(BF16)
                lc = left[pl.ds(pl.multiple_of(c * rows, rows), rows), :].astype(BF16)
                zc = jnp.zeros_like(lc)
                rhs = jnp.concatenate(
                    [jnp.concatenate([lc, zc], axis=1), jnp.concatenate([zc, lc], axis=1)], axis=0
                )
                work[pl.ds(c, PAD, stride=hid), :] = lax.dot_general(
                    lhs, rhs, NT, preferred_element_type=F32
                )
            return inner

        lax.fori_loop(0, hid // 8, channels, 0)
        for m in range(JD):
            send[p, m * hid : (m + 1) * hid, :] = work[m * hid : (m + 1) * hid, :].astype(BF16)

        @pl.when(p != z)
        def _():
            partial_copy(p).start()

        return carry

    lax.fori_loop(0, n_pos, stage, 0)

    def gates(g, carry):
        for t in range(2):
            x = gate_in[t, pl.ds(8 * g, 8)].reshape(8 * PAD, ch)
            mix = lax.dot_general(x, gweight[...], NN, preferred_element_type=F32)
            gate_val[t, pl.ds(8 * g, 8)] = sigmoid(mix).reshape(8, PAD, ch)
        return carry

    lax.fori_loop(0, rows // 8, gates, 0)

    ogain_v = jnp.broadcast_to(ogain[...], (2 * rows, hid)).T
    obias_v = jnp.broadcast_to(obias[...], (2 * rows, hid)).T
    zero_rows = jnp.zeros((2 * rows, ch), F32)
    for m in range(JD, PAD):
        update[pl.ds(m, 2 * rows, stride=PAD), :] = zero_rows

    for e in range(1, n_pos):
        partial_copy(xor(z, e, n_pos)).wait_recv()

    def finish(m, carry):
        here = pl.ds(pl.multiple_of(m * hid, hid), hid)
        total = send[z, here, :].astype(F32)
        for e in range(1, n_pos):
            total = total + recv[e, here, :].astype(F32)
        total = total.astype(BF16).astype(F32)
        centred = total - jnp.mean(total, axis=0, keepdims=True)
        spread = jnp.mean(centred * centred, axis=0, keepdims=True)
        normed = (centred * lax.rsqrt(spread + EPS) * ogain_v + obias_v).astype(BF16)
        update[pl.ds(m, 2 * rows, stride=PAD), :] = lax.dot_general(
            normed, oweight[...], TN, preferred_element_type=F32
        )
        return carry

    lax.fori_loop(0, JD, finish, 0)

    def write(g, carry):
        for t in range(2):
            at = pl.ds(pl.multiple_of((t * rows + 8 * g) * PAD, 8 * PAD), 8 * PAD)
            val = update[at, :].reshape(8, PAD, ch) * gate_val[t, pl.ds(8 * g, 8)]
            out[t, pl.ds(8 * g, 8)] = val.astype(BF16)
        return carry

    lax.fori_loop(0, rows // 8, write, 0)

    forward_copy(0).wait_send()
    for d in range(1, n_pos):
        right_copy(d).wait_send()
        forward_copy(d).wait_send()
        partial_copy(xor(z, d, n_pos)).wait_send()


def on_device(pair, lengths, gain, bias, lg, lv, rg, rv, ogain, obias, ow, gw):
    rows, cols, ch = pair.shape
    hid = lg.shape[1]
    n_blk = lax.axis_size("blk")
    n_pos = lax.axis_size("chan")
    assert n_blk == 2 * n_pos and cols == 2 * rows and n_pos & (n_pos - 1) == 0
    slot_size = rows * n_blk // lengths.shape[0]
    vmem = pl.BlockSpec(memory_space=pltpu.VMEM)
    dma = pltpu.SemaphoreType.DMA((n_pos,))
    block = (JD * hid, cols)
    out = pl.pallas_call(
        functools.partial(kernel, n_pos, slot_size),
        out_shape=jax.ShapeDtypeStruct((2, rows, PAD, ch), BF16),
        in_specs=[pl.BlockSpec(memory_space=pltpu.SMEM), pl.BlockSpec(memory_space=pl.ANY)]
        + [vmem] * 10,
        out_specs=vmem,
        scratch_shapes=[
            pltpu.VMEM((rows, cols, ch), BF16),
            pltpu.VMEM((4 * hid, ch), BF16),
            pltpu.VMEM((n_blk,) + block, BF16),
            pltpu.VMEM((hid * rows, cols), F32),
            pltpu.VMEM((hid * PAD, cols), F32),
            pltpu.VMEM((hid * PAD, cols), F32),
            pltpu.VMEM((PAD * hid, 2 * rows), F32),
            pltpu.VMEM((n_pos,) + block, BF16),
            pltpu.VMEM((n_pos,) + block, BF16),
            pltpu.VMEM((2, rows, PAD, ch), BF16),
            pltpu.VMEM((2, rows, PAD, ch), F32),
            pltpu.VMEM((2 * rows * PAD, ch), F32),
            pltpu.SemaphoreType.DMA((2,)),
            dma,
            dma,
            dma,
            dma,
            dma,
            dma,
        ],
        compiler_params=pltpu.CompilerParams(
            collective_id=0, has_side_effects=True, vmem_limit_bytes=60 * 2**20
        ),
    )(
        lengths,
        pair,
        gain.reshape(1, ch),
        bias.reshape(1, ch),
        lg,
        lv,
        rg,
        rv,
        ogain.reshape(1, hid),
        obias.reshape(1, hid),
        ow,
        gw,
    )
    return out[:, :, :JD].transpose(1, 0, 2, 3).reshape(rows, 2 * JD, ch)


def solution(mesh):
    in_specs = (P("blk", "chan", None),) + (P(),) * 11
    out_specs = P("blk", "chan", None)
    return jax.shard_map(
        on_device, mesh=mesh, in_specs=in_specs, out_specs=out_specs, check_vma=False
    )
```

time: 145 us -> 85.3 us (0.59)
  the two profiles are of different devices: /device:TPU:0 before, /device:TPU:7 now
where the time goes in v1:
time: 85.3 us; the launch traced here: 84.4 us
  Pallas kernels  82.5 us (97%)
  local copies, waits for them, and re-layouts  1.95 us (2%)
    pallas_call x1, Pallas kernels, on_device(): pl.pallas_call(functools.partial(kernel, n_pos, slot_size), out_shape=jax...  82.5 us
    transpose x2, local copies, waits for them, and re-layouts, on_device(): return out[:, :, :JD].transpose(1, 0, 2, 3).reshape(rows, 2 * JD, ch)  1.95 us

profile of v1, /device:TPU:7, one launch (start us, length us, event | category | flops | bytes accessed | tf_op | source)
XLA Modules:
  0.0 84.4 jit_solution(5487284207562801033)
XLA Ops:
  0.0 82.5 %shard_map.118 = bf16[2,64,16,128]{3,2,1,0:T(8,128)(2,1)} custom-call(s32[8]{0:T(128)} %lens.1, bf16[64,128,128]{2,1,0:T(8,128)(2,1)} %pair_hbm.1, f32[1,128]{1,0:T(1,128)} %bitcast.7, f32[1,128]{1,0:T(1,128)} %bitcast.8, bf16[128,128]{1,0:T(8,128)(2,1)} %lgate.1, bf16[128,128]{1,0:T(8,128)(2,1)} %lvalue.1, bf16[128,128]{1,0:T(8,128)(2,1)} %rgate.1, ...), custom_call_target="tpu_custom_call" | custom-call | tf_op jit(solution)/shard_map/pallas_call | solution.py:289
  82.5 1.1 %slice_bitcast_fusion = bf16[64,2,13,128]{3,2,0,1:T(8,128)(2,1)S(1)} fusion(bf16[2,64,16,128]{3,2,1,0:T(8,128)(2,1)} %shard_map.118), kind=kLoop, calls=%fused_computation | loop fusion | bytes 851968 | tf_op jit(solution)/shard_map/transpose | solution.py:333
  83.5 0.9 %copy.13 = bf16[64,2,13,128]{3,0,2,1:T(8,128)(2,1)} copy(bf16[64,2,13,128]{3,2,0,1:T(8,128)(2,1)S(1)} %slice_bitcast_fusion) | data formatting | bytes 851968 | tf_op jit(solution)/shard_map/transpose | solution.py:333

commit v2 on v1

--- a/solution.py
+++ b/solution.py
@@ -21,6 +21,14 @@
     total, bit = 0, 1
     while bit < n:
         total = total + bit * ((a // bit + b // bit) % 2)
+        bit *= 2
+    return total
+
+
+def reverse_bits(t, n):
+    total, bit = 0, 1
+    while bit < n:
+        total = total + (n // 2 // bit) * ((t // bit) % 2)
         bit *= 2
     return total
 
@@ -60,6 +68,7 @@
     r1,
     work,
     send,
+    own,
     recv,
     gate_in,
     gate_val,
@@ -148,31 +157,29 @@
         )
 
     forward_copy(0).start()
-    for d in range(1, n_pos):
-        right_copy(d).start()
+    for t in range(1, n_pos):
+        right_copy(reverse_bits(t, n_pos)).start()
 
     load_b.wait()
 
     def left_rows(t, carry):
-        i = 2 * t
-        normed = norm_rows(i, 2)
-        for u in range(2):
+        i = 8 * t
+        normed = norm_rows(i, 8)
+        for u in range(8):
             for g in range(2):
-                gate_in[g, i + u] = normed[u * cols + g * rows : u * cols + g * rows + PAD]
+                at = pl.ds(pl.multiple_of((i + u) * 2 * PAD, 2 * PAD) + g * JD, JD)
+                gate_in[at, :] = normed[
+                    u * cols + g * rows : u * cols + g * rows + JD
+                ].astype(F32)
         mix = lax.dot_general(weights[2 * hid :, :], normed, NT, preferred_element_type=F32)
         val = sigmoid(mix[:hid]) * mix[hid:]
-        for u in range(2):
-            left[pl.ds(i + u, hid, stride=rows), :] = val[:, u * cols : (u + 1) * cols] * (
+        for u in range(8):
+            left[pl.ds(i + u, hid, stride=rows + 8), :] = val[:, u * cols : (u + 1) * cols] * (
                 col_real * row_real(i + u)
             )
         return carry
 
-    lax.fori_loop(0, rows // 2, left_rows, 0)
-
-    zero_rows = jnp.zeros((hid, cols), F32)
-    for m in range(JD, PAD):
-        r0[pl.ds(m, hid, stride=PAD), :] = zero_rows
-        r1[pl.ds(m, hid, stride=PAD), :] = zero_rows
+    lax.fori_loop(0, rows // 8, left_rows, 0)
 
     def partial_copy(p):
         e = xor(z, p, n_pos)
@@ -184,7 +191,8 @@
             device_id={"chan": p},
         )
 
-    def stage(d, carry):
+    def stage(t, carry):
+        d = reverse_bits(t, n_pos)
         p = xor(q, d, n_pos)
 
         @pl.when(d > 0)
@@ -200,71 +208,70 @@
                 ].astype(F32)
 
         def channels(t, inner):
-            for u in range(8):
-                c = 8 * t + u
+            for u in range(32):
+                c = 32 * t + u
                 rr = pl.ds(pl.multiple_of(c * PAD, PAD), PAD)
-                lhs = jnp.concatenate([r0[rr, :], r1[rr, :]], axis=1).astype(BF16)
-                lc = left[pl.ds(pl.multiple_of(c * rows, rows), rows), :].astype(BF16)
-                zc = jnp.zeros_like(lc)
-                rhs = jnp.concatenate(
-                    [jnp.concatenate([lc, zc], axis=1), jnp.concatenate([zc, lc], axis=1)], axis=0
-                )
-                work[pl.ds(c, PAD, stride=hid), :] = lax.dot_general(
-                    lhs, rhs, NT, preferred_element_type=F32
-                )
+                lhs = jnp.concatenate([r0[rr, :], r1[rr, :]], axis=0).astype(BF16)
+                lc = left[pl.ds(pl.multiple_of(c * (rows + 8), 8), rows), :].astype(BF16)
+                o = lax.dot_general(lhs, lc, NT, preferred_element_type=F32)
+                work[pl.ds(c, PAD, stride=hid + 8), :] = jnp.concatenate([o[:PAD], o[PAD:]], axis=1)
             return inner
 
-        lax.fori_loop(0, hid // 8, channels, 0)
-        for m in range(JD):
-            send[p, m * hid : (m + 1) * hid, :] = work[m * hid : (m + 1) * hid, :].astype(BF16)
+        lax.fori_loop(0, hid // 32, channels, 0)
+        @pl.when(p == z)
+        def _():
+            for m in range(JD):
+                own[m * hid : (m + 1) * hid, :] = work[m * (hid + 8) : m * (hid + 8) + hid, :]
 
         @pl.when(p != z)
         def _():
+            for m in range(JD):
+                send[p, m * hid : (m + 1) * hid, :] = work[
+                    m * (hid + 8) : m * (hid + 8) + hid, :
+                ].astype(BF16)
             partial_copy(p).start()
 
         return carry
 
     lax.fori_loop(0, n_pos, stage, 0)
 
+    wide = 8 * 2 * PAD
+
     def gates(g, carry):
-        for t in range(2):
-            x = gate_in[t, pl.ds(8 * g, 8)].reshape(8 * PAD, ch)
-            mix = lax.dot_general(x, gweight[...], NN, preferred_element_type=F32)
-            gate_val[t, pl.ds(8 * g, 8)] = sigmoid(mix).reshape(8, PAD, ch)
+        at = pl.ds(pl.multiple_of(g * wide, wide), wide)
+        mix = lax.dot_general(
+            gate_in[at, :].astype(BF16), gweight[...], NN, preferred_element_type=F32
+        )
+        gate_val[at, :] = sigmoid(mix)
         return carry
 
     lax.fori_loop(0, rows // 8, gates, 0)
 
     ogain_v = jnp.broadcast_to(ogain[...], (2 * rows, hid)).T
     obias_v = jnp.broadcast_to(obias[...], (2 * rows, hid)).T
-    zero_rows = jnp.zeros((2 * rows, ch), F32)
-    for m in range(JD, PAD):
-        update[pl.ds(m, 2 * rows, stride=PAD), :] = zero_rows
-
     for e in range(1, n_pos):
         partial_copy(xor(z, e, n_pos)).wait_recv()
 
-    def finish(m, carry):
-        here = pl.ds(pl.multiple_of(m * hid, hid), hid)
-        total = send[z, here, :].astype(F32)
+    def finish(m):
+        here = slice(m * hid, (m + 1) * hid)
+        total = own[here, :]
         for e in range(1, n_pos):
             total = total + recv[e, here, :].astype(F32)
         total = total.astype(BF16).astype(F32)
         centred = total - jnp.mean(total, axis=0, keepdims=True)
         spread = jnp.mean(centred * centred, axis=0, keepdims=True)
         normed = (centred * lax.rsqrt(spread + EPS) * ogain_v + obias_v).astype(BF16)
-        update[pl.ds(m, 2 * rows, stride=PAD), :] = lax.dot_general(
-            normed, oweight[...], TN, preferred_element_type=F32
-        )
-        return carry
-
-    lax.fori_loop(0, JD, finish, 0)
+        val = lax.dot_general(normed, oweight[...], TN, preferred_element_type=F32)
+        for g in range(2):
+            update[pl.ds(g * JD + m, rows, stride=2 * PAD), :] = val[g * rows : (g + 1) * rows]
+
+    for m in range(JD):
+        finish(m)
 
     def write(g, carry):
-        for t in range(2):
-            at = pl.ds(pl.multiple_of((t * rows + 8 * g) * PAD, 8 * PAD), 8 * PAD)
-            val = update[at, :].reshape(8, PAD, ch) * gate_val[t, pl.ds(8 * g, 8)]
-            out[t, pl.ds(8 * g, 8)] = val.astype(BF16)
+        at = pl.ds(pl.multiple_of(g * wide, wide), wide)
+        val = (update[at, :] * gate_val[at, :]).reshape(8, 2 * PAD, ch)
+        out[pl.ds(pl.multiple_of(8 * g, 8), 8)] = val[:, : 2 * JD].astype(BF16)
         return carry
 
     lax.fori_loop(0, rows // 8, write, 0)
@@ -286,9 +293,9 @@
     vmem = pl.BlockSpec(memory_space=pltpu.VMEM)
     dma = pltpu.SemaphoreType.DMA((n_pos,))
     block = (JD * hid, cols)
-    out = pl.pallas_call(
+    return pl.pallas_call(
         functools.partial(kernel, n_pos, slot_size),
-        out_shape=jax.ShapeDtypeStruct((2, rows, PAD, ch), BF16),
+        out_shape=jax.ShapeDtypeStruct((rows, 2 * JD, ch), BF16),
         in_specs=[pl.BlockSpec(memory_space=pltpu.SMEM), pl.BlockSpec(memory_space=pl.ANY)]
         + [vmem] * 10,
         out_specs=vmem,
@@ -296,14 +303,15 @@
             pltpu.VMEM((rows, cols, ch), BF16),
             pltpu.VMEM((4 * hid, ch), BF16),
             pltpu.VMEM((n_blk,) + block, BF16),
-            pltpu.VMEM((hid * rows, cols), F32),
+            pltpu.VMEM((hid * (rows + 8), cols), F32),
             pltpu.VMEM((hid * PAD, cols), F32),
             pltpu.VMEM((hid * PAD, cols), F32),
-            pltpu.VMEM((PAD * hid, 2 * rows), F32),
+            pltpu.VMEM((PAD * (hid + 8), 2 * rows), F32),
             pltpu.VMEM((n_pos,) + block, BF16),
+            pltpu.VMEM(block, F32),
             pltpu.VMEM((n_pos,) + block, BF16),
-            pltpu.VMEM((2, rows, PAD, ch), BF16),
-            pltpu.VMEM((2, rows, PAD, ch), F32),
+            pltpu.VMEM((2 * rows * PAD, ch), F32),
+            pltpu.VMEM((2 * rows * PAD, ch), F32),
             pltpu.VMEM((2 * rows * PAD, ch), F32),
             pltpu.SemaphoreType.DMA((2,)),
             dma,
@@ -330,7 +338,6 @@
         ow,
         gw,
     )
-    return out[:, :, :JD].transpose(1, 0, 2, 3).reshape(rows, 2 * JD, ch)
 
 
 def solution(mesh):

time: 85.3 us -> 65.6 us (0.77)
  Pallas kernels: 82.5 us -> 63.4 us
    pallas_call x1, Pallas kernels: 82.5 us -> 63.4 us  [on_device(): pl.pallas_call(functools.partial(kernel, n_pos, slot_size), out_shape=jax...]
    pallas_call x0 -> x1, local copies, waits for them, and re-layouts: none -> 1.97 us  [on_device(): pl.pallas_call(functools.partial(kernel, n_pos, slot_size), out_shape=jax...]
    transpose x2 -> x0, local copies, waits for them, and re-layouts: 1.95 us -> none  [on_device(): return out[:, :, :JD].transpose(1, 0, 2, 3).reshape(rows, 2 * JD, ch)]
where the time goes in v2:
time: 65.6 us; the launch traced here: 65.4 us
  Pallas kernels  63.4 us (97%)
  local copies, waits for them, and re-layouts  1.97 us (3%)
    pallas_call x1, Pallas kernels, on_device(): pl.pallas_call(functools.partial(kernel, n_pos, slot_size), out_shape=jax...  63.4 us
    pallas_call x1, local copies, waits for them, and re-layouts, on_device(): pl.pallas_call(functools.partial(kernel, n_pos, slot_size), out_shape=jax...  1.97 us

profile of v2, /device:TPU:7, one launch (start us, length us, event | category | flops | bytes accessed | tf_op | source)
XLA Modules:
  0.0 65.4 jit_solution(12076307363405592)
XLA Ops:
  0.0 63.4 %shard_map.118 = bf16[64,26,128]{2,1,0:T(8,128)(2,1)} custom-call(s32[8]{0:T(128)} %lens.1, bf16[64,128,128]{2,1,0:T(8,128)(2,1)} %pair_hbm.1, f32[1,128]{1,0:T(1,128)} %bitcast.4, f32[1,128]{1,0:T(1,128)} %bitcast.5, bf16[128,128]{1,0:T(8,128)(2,1)} %lgate.1, bf16[128,128]{1,0:T(8,128)(2,1)} %lvalue.1, bf16[128,128]{1,0:T(8,128)(2,1)} %rgate.1, ...), custom_call_target="tpu_custom_call" | custom-call | tf_op jit(solution)/shard_map/pallas_call | solution.py:296
  63.4 2.0 %copy.13 = bf16[64,26,128]{2,0,1:T(8,128)(2,1)} copy(bf16[64,26,128]{2,1,0:T(8,128)(2,1)} %shard_map.118) | data formatting | bytes 851968 | tf_op jit(solution)/shard_map/pallas_call | solution.py:296

commit v3 on v2

--- a/solution.py
+++ b/solution.py
@@ -80,6 +80,9 @@
     fw_recv,
     ps_send,
     ps_recv,
+    relay,
+    rl_send,
+    rl_recv,
 ):
     rows, cols, ch = pair.shape
     hid = lgate.shape[1]
@@ -133,7 +136,8 @@
         right_all[blk, pl.ds(pl.multiple_of(m * hid, hid), hid), :] = val.astype(BF16)
         return carry
 
-    lax.fori_loop(0, JD, right_row, 0)
+    for m in range(JD):
+        right_row(m, 0)
 
     pl.semaphore_wait(barrier, 2 * (n_pos - 1) + 1)
 
@@ -191,50 +195,6 @@
             device_id={"chan": p},
         )
 
-    def stage(t, carry):
-        d = reverse_bits(t, n_pos)
-        p = xor(q, d, n_pos)
-
-        @pl.when(d > 0)
-        def _():
-            right_copy(d).wait_recv()
-            forward_copy(d).start()
-
-        forward_copy(d).wait_recv()
-        for g, dst in enumerate((r0, r1)):
-            for m in range(JD):
-                dst[pl.ds(m, hid, stride=PAD), :] = right_all[
-                    2 * p + g, m * hid : (m + 1) * hid, :
-                ].astype(F32)
-
-        def channels(t, inner):
-            for u in range(32):
-                c = 32 * t + u
-                rr = pl.ds(pl.multiple_of(c * PAD, PAD), PAD)
-                lhs = jnp.concatenate([r0[rr, :], r1[rr, :]], axis=0).astype(BF16)
-                lc = left[pl.ds(pl.multiple_of(c * (rows + 8), 8), rows), :].astype(BF16)
-                o = lax.dot_general(lhs, lc, NT, preferred_element_type=F32)
-                work[pl.ds(c, PAD, stride=hid + 8), :] = jnp.concatenate([o[:PAD], o[PAD:]], axis=1)
-            return inner
-
-        lax.fori_loop(0, hid // 32, channels, 0)
-        @pl.when(p == z)
-        def _():
-            for m in range(JD):
-                own[m * hid : (m + 1) * hid, :] = work[m * (hid + 8) : m * (hid + 8) + hid, :]
-
-        @pl.when(p != z)
-        def _():
-            for m in range(JD):
-                send[p, m * hid : (m + 1) * hid, :] = work[
-                    m * (hid + 8) : m * (hid + 8) + hid, :
-                ].astype(BF16)
-            partial_copy(p).start()
-
-        return carry
-
-    lax.fori_loop(0, n_pos, stage, 0)
-
     wide = 8 * 2 * PAD
 
     def gates(g, carry):
@@ -245,18 +205,115 @@
         gate_val[at, :] = sigmoid(mix)
         return carry
 
+    last = n_pos - 1
+    half = n_pos // 2
+
+    def relayed(source, p):
+        ends = ((source == 0) & (p >= half)) | ((source == last) & (p < half))
+        return ends & ((p + q) % 2 == 1)
+
+    next_in = jnp.where(z == 0, 1, jnp.where(z == last, last - 1, -1))
+    behind = jnp.where(z == 1, 0, jnp.where(z == last - 1, last, -1))
+
+    def relay_copy(p):
+        return pltpu.make_async_remote_copy(
+            src_ref=send.at[p],
+            dst_ref=relay.at[p],
+            send_sem=rl_send.at[p],
+            recv_sem=rl_recv.at[p],
+            device_id={"chan": jnp.where(z < half, 1, last - 1)},
+        )
+
+    def stage(t, carry):
+        d = reverse_bits(t, n_pos)
+        p = xor(q, d, n_pos)
+
+        @pl.when(d > 0)
+        def _():
+            right_copy(d).wait_recv()
+            forward_copy(d).start()
+
+        forward_copy(d).wait_recv()
+        for g, dst in enumerate((r0, r1)):
+            for m in range(JD):
+                dst[pl.ds(m, hid, stride=PAD + 8), :] = right_all[
+                    2 * p + g, m * hid : (m + 1) * hid, :
+                ].astype(F32)
+
+        def channels(t, inner):
+            for u in range(32):
+                c = 32 * t + u
+                rr = pl.ds(pl.multiple_of(c * (PAD + 8), 8), PAD)
+                lhs = jnp.concatenate([r0[rr, :], r1[rr, :]], axis=0).astype(BF16)
+                lc = left[pl.ds(pl.multiple_of(c * (rows + 8), 8), rows), :].astype(BF16)
+                o = lax.dot_general(lhs, lc, NT, preferred_element_type=F32)
+                work[pl.ds(c, PAD, stride=hid + 8), :] = jnp.concatenate([o[:PAD], o[PAD:]], axis=1)
+            return inner
+
+        lax.fori_loop(0, hid // 32, channels, 0)
+        @pl.when(p == z)
+        def _():
+            for m in range(JD):
+                own[m * hid : (m + 1) * hid, :] = work[m * (hid + 8) : m * (hid + 8) + hid, :]
+
+        @pl.when(p != z)
+        def _():
+            for m in range(JD):
+                send[p, m * hid : (m + 1) * hid, :] = work[
+                    m * (hid + 8) : m * (hid + 8) + hid, :
+                ].astype(BF16)
+
+            @pl.when(relayed(z, p))
+            def _():
+                relay_copy(p).start()
+
+            later = (p == next_in) | relayed(behind, p)
+
+            @pl.when(jnp.logical_not(relayed(z, p) | later))
+            def _():
+                partial_copy(p).start()
+
+        return carry
+
+    lax.fori_loop(0, n_pos, stage, 0)
+
+    @pl.when(next_in >= 0)
+    def _():
+        partial_copy(next_in).start()
+
+    def pass_on(t, carry):
+        p = xor(q, reverse_bits(half + t, n_pos), n_pos)
+
+        @pl.when(relayed(behind, p))
+        def _():
+            relay_copy(p).wait_recv()
+            for m in range(JD):
+                here = slice(m * hid, (m + 1) * hid)
+                send[p, here, :] = (
+                    send[p, here, :].astype(F32) + relay[p, here, :].astype(F32)
+                ).astype(BF16)
+            partial_copy(p).start()
+
+        return carry
+
     lax.fori_loop(0, rows // 8, gates, 0)
+    lax.fori_loop(0, half, pass_on, 0)
 
     ogain_v = jnp.broadcast_to(ogain[...], (2 * rows, hid)).T
     obias_v = jnp.broadcast_to(obias[...], (2 * rows, hid)).T
     for e in range(1, n_pos):
-        partial_copy(xor(z, e, n_pos)).wait_recv()
+        source = xor(z, e, n_pos)
+
+        @pl.when(jnp.logical_not(relayed(source, z)))
+        def _():
+            partial_copy(source).wait_recv()
 
     def finish(m):
         here = slice(m * hid, (m + 1) * hid)
         total = own[here, :]
         for e in range(1, n_pos):
-            total = total + recv[e, here, :].astype(F32)
+            more = recv[e, here, :].astype(F32)
+            total = total + jnp.where(relayed(xor(z, e, n_pos), z), 0.0, more)
         total = total.astype(BF16).astype(F32)
         centred = total - jnp.mean(total, axis=0, keepdims=True)
         spread = jnp.mean(centred * centred, axis=0, keepdims=True)
@@ -280,7 +337,15 @@
     for d in range(1, n_pos):
         right_copy(d).wait_send()
         forward_copy(d).wait_send()
-        partial_copy(xor(z, d, n_pos)).wait_send()
+        target = xor(z, d, n_pos)
+
+        @pl.when(relayed(z, target))
+        def _():
+            relay_copy(target).wait_send()
+
+        @pl.when(jnp.logical_not(relayed(z, target)))
+        def _():
+            partial_copy(target).wait_send()
 
 
 def on_device(pair, lengths, gain, bias, lg, lv, rg, rv, ogain, obias, ow, gw):
@@ -288,7 +353,7 @@
     hid = lg.shape[1]
     n_blk = lax.axis_size("blk")
     n_pos = lax.axis_size("chan")
-    assert n_blk == 2 * n_pos and cols == 2 * rows and n_pos & (n_pos - 1) == 0
+    assert n_blk == 2 * n_pos and cols == 2 * rows and n_pos >= 4 and n_pos & (n_pos - 1) == 0
     slot_size = rows * n_blk // lengths.shape[0]
     vmem = pl.BlockSpec(memory_space=pltpu.VMEM)
     dma = pltpu.SemaphoreType.DMA((n_pos,))
@@ -304,8 +369,8 @@
             pltpu.VMEM((4 * hid, ch), BF16),
             pltpu.VMEM((n_blk,) + block, BF16),
             pltpu.VMEM((hid * (rows + 8), cols), F32),
-            pltpu.VMEM((hid * PAD, cols), F32),
-            pltpu.VMEM((hid * PAD, cols), F32),
+            pltpu.VMEM((hid * (PAD + 8), cols), F32),
+            pltpu.VMEM((hid * (PAD + 8), cols), F32),
             pltpu.VMEM((PAD * (hid + 8), 2 * rows), F32),
             pltpu.VMEM((n_pos,) + block, BF16),
             pltpu.VMEM(block, F32),
@@ -318,6 +383,9 @@
             dma,
             dma,
             dma,
+            dma,
+            dma,
+            pltpu.VMEM((n_pos,) + block, BF16),
             dma,
             dma,
         ],

time: 65.6 us -> 54.9 us (0.84)
  Pallas kernels: 63.4 us -> 52.6 us
    pallas_call x1, Pallas kernels: 63.4 us -> 52.6 us  [on_device(): pl.pallas_call(functools.partial(kernel, n_pos, slot_size), out_shape=jax...]
where the time goes in v3:
time: 54.9 us; the launch traced here: 54.6 us
  Pallas kernels  52.6 us (96%)
  local copies, waits for them, and re-layouts  1.97 us (4%)
    pallas_call x1, Pallas kernels, on_device(): pl.pallas_call(functools.partial(kernel, n_pos, slot_size), out_shape=jax...  52.6 us
    pallas_call x1, local copies, waits for them, and re-layouts, on_device(): pl.pallas_call(functools.partial(kernel, n_pos, slot_size), out_shape=jax...  1.97 us

profile of v3, /device:TPU:7, one launch (start us, length us, event | category | flops | bytes accessed | tf_op | source)
XLA Modules:
  0.0 54.6 jit_solution(18087132121671675591)
XLA Ops:
  0.0 52.6 %shard_map.118 = bf16[64,26,128]{2,1,0:T(8,128)(2,1)} custom-call(s32[8]{0:T(128)} %lens.1, bf16[64,128,128]{2,1,0:T(8,128)(2,1)} %pair_hbm.1, f32[1,128]{1,0:T(1,128)} %bitcast.4, f32[1,128]{1,0:T(1,128)} %bitcast.5, bf16[128,128]{1,0:T(8,128)(2,1)} %lgate.1, bf16[128,128]{1,0:T(8,128)(2,1)} %lvalue.1, bf16[128,128]{1,0:T(8,128)(2,1)} %rgate.1, ...), custom_call_target="tpu_custom_call" | custom-call | tf_op jit(solution)/shard_map/pallas_call | solution.py:361
  52.6 2.0 %copy.13 = bf16[64,26,128]{2,0,1:T(8,128)(2,1)} copy(bf16[64,26,128]{2,1,0:T(8,128)(2,1)} %shard_map.118) | data formatting | bytes 851968 | tf_op jit(solution)/shard_map/pallas_call | solution.py:361
